TPU v7x, 8 devices: a whole 2x2x1 slice. The times are simulated.
8 devices in a mesh: dp: 1 (over z), tp: 8 (over y, x, core).
Axes of the slice: x: 2, y: 2, z: 1, core: 2. Of those that a mesh axis runs over, the one named last changes fastest.
Arguments:
- hidden: bfloat16 [1, 16, 2048], P('dp')
- norm_w: bfloat16 [2048], replicated
- embedding: bfloat16 [256000, 2048], P('tp')
- draft_ids: int32 [1, 16], P('dp')
Outputs:
- output 1: float32 [1, 16], P('dp')
- output 2: float32 [1, 16], P('dp')
All inputs are finite; a program needn't handle non-finite values.
Results may differ from a plain program's by a relative error of at most 0.001.
Values sent between devices are 32-bit elements.
A program may use at most 1 GiB of HBM per device.

v0:
```python
import jax
import jax.numpy as jnp
from jax import lax
from jax.sharding import PartitionSpec as P, NamedSharding

EPS = 1e-6


def solution(mesh):
    def local_part(hidden, norm_w, embedding, draft_ids):
        shard_rows = embedding.shape[0]
        offset = lax.axis_index("tp") * shard_rows
        x_float = hidden.astype(jnp.float32)
        mean_sq = jnp.mean(x_float * x_float, axis=-1, keepdims=True)
        normed = (x_float * lax.rsqrt(mean_sq + EPS) * (1.0 + norm_w.astype(jnp.float32))).astype(jnp.bfloat16)
        logits = jnp.einsum("bgd,vd->bgv", normed, embedding, preferred_element_type=jnp.float32)
        local_max = jnp.max(logits, axis=-1)
        row_max = lax.pmax(local_max, "tp")
        exp_shift = jnp.exp(logits - row_max[..., None])
        exp_total = lax.psum(jnp.sum(exp_shift, axis=-1), "tp")
        weighted = lax.psum(jnp.sum(exp_shift * logits, axis=-1), "tp")
        local_ids = draft_ids - offset
        is_owned = (local_ids >= 0) & (local_ids < shard_rows)
        safe_ids = jnp.clip(local_ids, 0, shard_rows - 1)
        local_pick = jnp.take_along_axis(logits, safe_ids[..., None], axis=-1)[..., 0]
        picked = lax.psum(jnp.where(is_owned, local_pick, 0.0), "tp")
        log_norm = row_max + jnp.log(exp_total)
        return picked - log_norm, log_norm - weighted / exp_total

    return jax.shard_map(local_part, mesh=mesh, in_specs=(P("dp", None, None), P(None), P("tp", None), P("dp", None)), out_specs=(P("dp", None), P("dp", None)), check_vma=False)
```

profile of v0, /device:TPU:0, one launch (start us, length us, event | category | flops | bytes accessed | tf_op | source)
XLA Modules:
  0.0 98.4 jit_solution(5582607189993697462)
XLA Ops:
  0.6 0.7 convert_add_fusion
  1.3 1.0 fusion.1
  2.3 45.8 %fusion.10 = (f32[16]{0:T(128)S(1)}, f32[16,32000]{1,0:T(8,128)S(1)}) fusion(bf16[32000,2048]{1,0:T(8,128)(2,1)} %param.6, bf16[1,16,2048]{2,1,0:T(8,128)(2,1)} %param.4, f32[2048]{0:T(1024)S(1)} %convert_add_fusion, f32[16]{0:T(128)S(1)} %add_rsqrt_fusion), kind=kOutput, calls=%fused_computation.24 | convolution fusion | flops 2097795072 | bytes 133193856 | tf_op jit(solution)/shard_map/bgd,vd->bgv/dot_general | solution.py:16
  48.1 0.0 copy-start
  48.1 25.1 %pmax.7 = f32[1,16]{1,0:T(1,128)S(1)} all-reduce(f32[1,16]{1,0:T(1,128)S(1)} %bitcast.24), channel_id=1, replica_groups=mesh['dp'=1,'tp'=8] {'tp'}, use_global_device_ids=true, to_apply=%region_3.0 | all-reduce | flops 16 | bytes 128 | tf_op jit(solution)/shard_map/pmax | solution.py:18
  73.2 0.9 multiply_reduce_fusion
  74.1 0.0 copy-done
  74.1 0.7 gather_fusion
  74.8 23.1 %all-reduce = (f32[1,16]{1,0:T(1,128)S(1)}, f32[1,16]{1,0:T(1,128)S(1)}, f32[1,16]{1,0:T(1,128)S(1)}) all-reduce(f32[1,16]{1,0:T(1,128)S(1)} %and_select_fusion.1, f32[1,16]{1,0:T(1,128)S(1)} %bitcast.23, f32[1,16]{1,0:T(1,128)S(1)} %bitcast.22), channel_id=1, replica_groups=mesh['dp'=1,'tp'=8] {'tp'}, use_global_device_ids=true, to_apply=%region_1.0 | all-reduce | flops 48 | bytes 384 | tf_op jit(solution)/shard_map/psum | solution.py:26
  97.9 0.5 divide_subtract_fusion
  (6 shorter events, 0.1 us)
Async XLA Ops:
  48.1 26.0 %copy-start = (s32[1,16]{1,0:T(1,128)S(1)}, s32[1,16]{1,0:T(1,128)}, u32[]{:S(2)}) copy-start(s32[1,16]{1,0:T(1,128)} %param.7) | copy-start | bytes 196
where the time goes:
time: 98.8 us; the launch traced here: 98.4 us
  blocking collectives  48.1 us (49%)
  matrix products  45.8 us (46%)
  other arithmetic  3.11 us (3%)
    dot_general x1, matrix products, local_part(): jnp.einsum('bgd,vd->bgv', normed, embedding, preferred_element_type=jnp.f...  45.8 us
    pmax x1, blocking collectives, local_part(): row_max = lax.pmax(local_max, 'tp')  25.1 us
    psum x1, blocking collectives, local_part(): picked = lax.psum(jnp.where(is_owned, local_pick, 0.0), 'tp')  23.1 us

commit v1 on v0

v1 whole, which is shorter than its diff:
```python
import functools
import jax
import jax.numpy as jnp
from jax import lax
from jax.experimental import pallas as pl
from jax.experimental.pallas import tpu as pltpu
from jax.sharding import PartitionSpec as P

EPS = 1e-6
LANES = 128
BLOCK = 1280
DEPTH = 8
LOW = -3.0e38
MESH = pl.DeviceIdType.MESH


def head_kernel(n_dev, x_hbm, w_hbm, ids_hbm, e_hbm, lp_ref, en_ref,
                x_ref, w_ref, ids_ref, h_ref, buf, z_ref, stat, mine, got,
                small_sem, ring_sem, send_sem, recv_sem):
    rows = e_hbm.shape[0]
    pos = x_ref.shape[1]
    steps = rows // BLOCK
    me = lax.axis_index("tp")
    barrier = pltpu.get_barrier_semaphore()

    small = [pltpu.make_async_copy(s, d, small_sem.at[k])
             for k, (s, d) in enumerate(((x_hbm, x_ref), (w_hbm, w_ref), (ids_hbm, ids_ref)))]
    for c in small:
        c.start()

    def fetch(i):
        slot = lax.rem(i, DEPTH)
        return pltpu.make_async_copy(e_hbm.at[pl.ds(i * BLOCK, BLOCK), :], buf.at[slot], ring_sem.at[slot])

    for i in range(DEPTH - 1):
        fetch(i).start()
    for d in range(1, n_dev):
        pl.semaphore_signal(barrier, inc=1, device_id={"tp": lax.rem(me + d, n_dev)}, device_id_type=MESH)
    for c in small:
        c.wait()

    x = x_ref[0].astype(jnp.float32)
    r = lax.rsqrt(jnp.mean(x * x, axis=-1, keepdims=True) + EPS)
    gain = 1.0 + w_ref[...].astype(jnp.float32)
    for c in range(x.shape[1] // LANES):
        cols = slice(c * LANES, (c + 1) * LANES)
        h_ref[:, cols] = (x[:, cols] * r * gain[c:c + 1, :]).astype(jnp.bfloat16)

    sub = lax.broadcasted_iota(jnp.int32, (pos, pos), 0)
    lan = lax.broadcasted_iota(jnp.int32, (pos, pos), 1)
    eye = sub == lan
    ids_row = jnp.broadcast_to(ids_ref[...], (pos, pos)).astype(jnp.float32)
    ids_col = jnp.sum(jnp.where(eye, ids_row, 0.0), axis=1, keepdims=True).astype(jnp.int32)
    ids_rel = ids_col - me * rows - lax.broadcasted_iota(jnp.int32, (pos, LANES), 1)

    stat[0] = jnp.full((pos, LANES), LOW, jnp.float32)
    for k in range(1, 4):
        stat[k] = jnp.zeros((pos, LANES), jnp.float32)

    def logits(i):
        return lax.dot_general(h_ref[...], buf[lax.rem(i, DEPTH)], (((1,), (1,)), ((), ())),
                               preferred_element_type=jnp.float32)

    def fold(i):
        tiles = [z_ref[:, j * LANES:(j + 1) * LANES] for j in range(BLOCK // LANES)]
        m_old = stat[0]
        m_new = functools.reduce(jnp.maximum, tiles, m_old)
        scale = jnp.exp(m_old - m_new)
        s, a, p = stat[1] * scale, stat[2] * scale, stat[3]
        for j, t in enumerate(tiles):
            e = jnp.exp(t - m_new)
            s += e
            a += e * t
            p += jnp.where(ids_rel == i * BLOCK + j * LANES, t, 0.0)
        stat[0], stat[1], stat[2], stat[3] = m_new, s, a, p

    fetch(DEPTH - 1).start()
    fetch(0).wait()
    z_ref[...] = logits(0)

    def step(i, _):
        fetch(i).wait()
        nxt = i + DEPTH - 1

        @pl.when(nxt < steps)
        def _():
            fetch(nxt).start()

        z = logits(i)
        fold(i - 1)
        z_ref[...] = z
        return 0

    lax.fori_loop(1, steps, step, 0)
    fold(steps - 1)

    m_l, s_l, a_l, p_l = stat[0], stat[1], stat[2], stat[3]
    m_t, s_t, a_t, p_t = m_l.T, s_l.T, a_l.T, p_l.T
    m = jnp.max(m_t, axis=0, keepdims=True)
    wgt = jnp.exp(m_t - m)
    for k, v in enumerate((m, jnp.sum(s_t * wgt, axis=0, keepdims=True),
                           jnp.sum(a_t * wgt, axis=0, keepdims=True), jnp.sum(p_t, axis=0, keepdims=True))):
        mine[k:k + 1, :pos] = v
    got[me] = mine[...]
    pl.semaphore_wait(barrier, n_dev - 1)

    def send(d):
        peer = lax.rem(me + d, n_dev)
        return pltpu.make_async_remote_copy(
            src_ref=mine, dst_ref=got.at[me], send_sem=send_sem.at[d], recv_sem=recv_sem.at[me],
            device_id={"tp": peer}, device_id_type=MESH)

    def arrive(d):
        peer = lax.rem(me + d, n_dev)
        return pltpu.make_async_remote_copy(
            src_ref=mine, dst_ref=got.at[peer], send_sem=send_sem.at[d], recv_sem=recv_sem.at[peer],
            device_id={"tp": peer}, device_id_type=MESH)

    sends = [send(d) for d in range(1, n_dev)]
    for c in sends:
        c.start()
    for d in range(1, n_dev):
        arrive(d).wait_recv()
    ms = [got[d, 0:1, :pos] for d in range(n_dev)]
    top = functools.reduce(jnp.maximum, ms)
    ws = [jnp.exp(v - top) for v in ms]
    total = sum(got[d, 1:2, :pos] * ws[d] for d in range(n_dev))
    weighted = sum(got[d, 2:3, :pos] * ws[d] for d in range(n_dev))
    picked = sum(got[d, 3:4, :pos] for d in range(n_dev))
    log_norm = top + jnp.log(total)
    lp_ref[...] = picked - log_norm
    en_ref[...] = log_norm - weighted / total
    for c in sends:
        c.wait_send()


def solution(mesh):
    n_dev = mesh.shape["tp"]

    def local_part(hidden, norm_w, embedding, draft_ids):
        _, pos, width = hidden.shape
        hbm = pl.BlockSpec(memory_space=pltpu.HBM)
        vmem = pl.BlockSpec(memory_space=pltpu.VMEM)
        return pl.pallas_call(
            functools.partial(head_kernel, n_dev),
            out_shape=[jax.ShapeDtypeStruct((1, pos), jnp.float32)] * 2,
            in_specs=[hbm] * 4,
            out_specs=[vmem] * 2,
            scratch_shapes=[
                pltpu.VMEM((1, pos, width), jnp.bfloat16),
                pltpu.VMEM((width // LANES, LANES), jnp.bfloat16),
                pltpu.VMEM((1, pos), jnp.int32),
                pltpu.VMEM((pos, width), jnp.bfloat16),
                pltpu.VMEM((DEPTH, BLOCK, width), jnp.bfloat16),
                pltpu.VMEM((pos, BLOCK), jnp.float32),
                pltpu.VMEM((4, pos, LANES), jnp.float32),
                pltpu.VMEM((8, LANES), jnp.float32),
                pltpu.VMEM((n_dev, 8, LANES), jnp.float32),
                pltpu.SemaphoreType.DMA((3,)),
                pltpu.SemaphoreType.DMA((DEPTH,)),
                pltpu.SemaphoreType.DMA((n_dev,)),
                pltpu.SemaphoreType.DMA((n_dev,)),
            ],
            compiler_params=pltpu.CompilerParams(
                collective_id=0, has_side_effects=True, vmem_limit_bytes=60 * 2**20),
            cost_estimate=pl.CostEstimate(flops=2 * pos * embedding.size, bytes_accessed=2 * embedding.size,
                                          transcendentals=pos * embedding.shape[0]),
            name="head",
        )(hidden, norm_w.reshape(width // LANES, LANES), draft_ids, embedding)

    return jax.shard_map(local_part, mesh=mesh,
                         in_specs=(P("dp", None, None), P(None), P("tp", None), P("dp", None)),
                         out_specs=(P("dp", None), P("dp", None)), check_vma=False)
```

time: 98.8 us -> 56.6 us (0.57)
  Pallas kernels: 0 us -> 53.6 us
  blocking collectives: 48.1 us -> 0 us
  matrix products: 45.8 us -> 0 us
  other arithmetic: 3.11 us -> 0 us
  local copies, waits for them, and re-layouts: 0.69 us -> 2.25 us
    pallas_call x0 -> x1, Pallas kernels: none -> 53.6 us  [local_part(): pl.pallas_call(functools.partial(head_kernel, n_dev), out_shape=[jax.Shap...]
    dot_general x1 -> x0, matrix products: 45.8 us -> none  [local_part(): jnp.einsum('bgd,vd->bgv', normed, embedding, preferred_element_type=jnp.f...]
    pmax x1 -> x0, blocking collectives: 25.1 us -> none  [local_part(): row_max = lax.pmax(local_max, 'tp')]
    psum x1 -> x0, blocking collectives: 23.1 us -> none  [local_part(): picked = lax.psum(jnp.where(is_owned, local_pick, 0.0), 'tp')]
    unnamed x3 -> x2, local copies, waits for them, and re-layouts: 0.01 us -> 2.25 us
    reduce_sum x2 -> x0, other arithmetic: 1.85 us -> none  [the longest x1 0.97 us: local_part(): mean_sq = jnp.mean(x_float * x_float, axis=-1, keepdims=True)]
where the time goes in v1:
time: 56.6 us; the launch traced here: 56.5 us
  Pallas kernels  53.6 us (95%)
  local copies, waits for them, and re-layouts  2.25 us (4%)
  between operations  0.64 us (1%)
    pallas_call x1, Pallas kernels, local_part(): pl.pallas_call(functools.partial(head_kernel, n_dev), out_shape=[jax.Shap...  53.6 us
    unnamed x2, local copies, waits for them, and re-layouts  2.25 us

profile of v1, /device:TPU:0, one launch (start us, length us, event | category | flops | bytes accessed | tf_op | source)
XLA Modules:
  0.0 56.5 jit_solution(8502131699007265449)
XLA Ops:
  0.6 53.6 %head.1 = (f32[1,16]{1,0:T(1,128)}, f32[1,16]{1,0:T(1,128)}) custom-call(bf16[1,16,2048]{2,1,0:T(8,128)(2,1)} %x_hbm.1, bf16[16,128]{1,0:T(8,128)(2,1)} %bitcast.1, s32[1,16]{1,0:T(1,128)} %ids_hbm.1, bf16[32000,2048]{1,0:T(8,128)(2,1)} %e_hbm.1), custom_call_target="tpu_custom_call" | custom-call | flops 2097152000 | bytes 131072000 | tf_op jit(solution)/shard_map/head/pallas_call | solution.py:144
  54.2 1.1 %copy.8 = f32[1,16]{1,0:T(1,128)} copy(f32[1,16]{1,0:T(1,128)} %get-tuple-element.4) | data formatting | bytes 128
  55.3 1.1 %copy.9 = f32[1,16]{1,0:T(1,128)} copy(f32[1,16]{1,0:T(1,128)} %get-tuple-element.5) | data formatting | bytes 128

commit v2 on v1

--- a/solution.py
+++ b/solution.py
@@ -14,7 +14,7 @@
 MESH = pl.DeviceIdType.MESH
 
 
-def head_kernel(n_dev, x_hbm, w_hbm, ids_hbm, e_hbm, lp_ref, en_ref,
+def head_kernel(n_dev, x_hbm, w_hbm, ids_hbm, e_hbm, out_ref,
                 x_ref, w_ref, ids_ref, h_ref, buf, z_ref, stat, mine, got,
                 small_sem, ring_sem, send_sem, recv_sem):
     rows = e_hbm.shape[0]
@@ -127,9 +127,8 @@
     total = sum(got[d, 1:2, :pos] * ws[d] for d in range(n_dev))
     weighted = sum(got[d, 2:3, :pos] * ws[d] for d in range(n_dev))
     picked = sum(got[d, 3:4, :pos] for d in range(n_dev))
-    log_norm = top + jnp.log(total)
-    lp_ref[...] = picked - log_norm
-    en_ref[...] = log_norm - weighted / total
+    for k, v in enumerate((top, total, weighted, picked)):
+        out_ref[k:k + 1, :pos] = v
     for c in sends:
         c.wait_send()
 
@@ -141,11 +140,11 @@
         _, pos, width = hidden.shape
         hbm = pl.BlockSpec(memory_space=pltpu.HBM)
         vmem = pl.BlockSpec(memory_space=pltpu.VMEM)
-        return pl.pallas_call(
+        out = pl.pallas_call(
             functools.partial(head_kernel, n_dev),
-            out_shape=[jax.ShapeDtypeStruct((1, pos), jnp.float32)] * 2,
+            out_shape=pltpu.VMEM((8, LANES), jnp.float32),
             in_specs=[hbm] * 4,
-            out_specs=[vmem] * 2,
+            out_specs=vmem,
             scratch_shapes=[
                 pltpu.VMEM((1, pos, width), jnp.bfloat16),
                 pltpu.VMEM((width // LANES, LANES), jnp.bfloat16),
@@ -167,6 +166,9 @@
                                           transcendentals=pos * embedding.shape[0]),
             name="head",
         )(hidden, norm_w.reshape(width // LANES, LANES), draft_ids, embedding)
+        top, total, weighted, picked = (out[k:k + 1, :pos] for k in range(4))
+        log_norm = top + jnp.log(total)
+        return picked - log_norm, log_norm - weighted / total
 
     return jax.shard_map(local_part, mesh=mesh,
                          in_specs=(P("dp", None, None), P(None), P("tp", None), P("dp", None)),

time: 56.6 us -> 54.3 us (0.959)
  local copies, waits for them, and re-layouts: 2.25 us -> 0 us
  Pallas kernels: 53.6 us -> 53 us
    unnamed x2 -> x0, local copies, waits for them, and re-layouts: 2.25 us -> none
where the time goes in v2:
time: 54.3 us; the launch traced here: 54.2 us
  Pallas kernels  53 us (98%)
  between operations  0.64 us (1%)
    pallas_call x1, Pallas kernels, local_part(): pl.pallas_call(functools.partial(head_kernel, n_dev), out_shape=pltpu.VME...  53 us

profile of v2, /device:TPU:0, one launch (start us, length us, event | category | flops | bytes accessed | tf_op | source)
XLA Modules:
  0.0 54.2 jit_solution(14838826960199951477)
XLA Ops:
  0.6 53.0 %head.1 = f32[8,128]{1,0:T(8,128)S(1)} custom-call(bf16[1,16,2048]{2,1,0:T(8,128)(2,1)} %x_hbm.1, bf16[16,128]{1,0:T(8,128)(2,1)} %bitcast.1, s32[1,16]{1,0:T(1,128)} %ids_hbm.1, bf16[32000,2048]{1,0:T(8,128)(2,1)} %e_hbm.1), custom_call_target="tpu_custom_call" | custom-call | flops 2097152000 | bytes 131072000 | tf_op jit(solution)/shard_map/head/pallas_call | solution.py:143
  53.7 0.5 divide_subtract_fusion

commit v3 on v2

v3 whole, which is shorter than its diff:
```python
import functools
import jax
import jax.numpy as jnp
from jax import lax
from jax.experimental import pallas as pl
from jax.experimental.pallas import tpu as pltpu
from jax.sharding import PartitionSpec as P

EPS = 1e-6
LANES = 128
BLOCK = 1280
DEPTH = 8
LOW = -3.0e38
MESH = pl.DeviceIdType.MESH


def stream_kernel(x_hbm, w_hbm, ids_hbm, e_hbm, out_ref,
                  x_ref, w_ref, ids_ref, h_ref, buf, z_ref, stat, small_sem, ring_sem):
    rows = e_hbm.shape[0]
    pos = x_ref.shape[1]
    steps = rows // BLOCK

    small = [pltpu.make_async_copy(s, d, small_sem.at[k])
             for k, (s, d) in enumerate(((x_hbm, x_ref), (w_hbm, w_ref), (ids_hbm, ids_ref)))]
    for c in small:
        c.start(priority=0)

    def fetch(i):
        slot = lax.rem(i, DEPTH)
        return pltpu.make_async_copy(e_hbm.at[pl.ds(i * BLOCK, BLOCK), :], buf.at[slot], ring_sem.at[slot])

    for i in range(DEPTH):
        fetch(i).start(priority=1)
    for c in small:
        c.wait()

    x = x_ref[0].astype(jnp.float32)
    r = lax.rsqrt(jnp.mean(x * x, axis=-1, keepdims=True) + EPS)
    gain = 1.0 + w_ref[...].astype(jnp.float32)
    for c in range(x.shape[1] // LANES):
        cols = slice(c * LANES, (c + 1) * LANES)
        h_ref[:, cols] = (x[:, cols] * r * gain[c:c + 1, :]).astype(jnp.bfloat16)

    sub = lax.broadcasted_iota(jnp.int32, (pos, pos), 0)
    lan = lax.broadcasted_iota(jnp.int32, (pos, pos), 1)
    ids_row = jnp.broadcast_to(ids_ref[...], (pos, pos)).astype(jnp.float32)
    ids_col = jnp.sum(jnp.where(sub == lan, ids_row, 0.0), axis=1, keepdims=True).astype(jnp.int32)
    ids_rel = ids_col - lax.axis_index("tp") * rows - lax.broadcasted_iota(jnp.int32, (pos, LANES), 1)

    stat[0] = jnp.full((pos, LANES), LOW, jnp.float32)
    for k in range(1, 4):
        stat[k] = jnp.zeros((pos, LANES), jnp.float32)

    def logits(i):
        return lax.dot_general(h_ref[...], buf[lax.rem(i, DEPTH)], (((1,), (1,)), ((), ())),
                               preferred_element_type=jnp.float32)

    def fold(i):
        tiles = [z_ref[:, j * LANES:(j + 1) * LANES] for j in range(BLOCK // LANES)]
        m_old = stat[0]
        m_new = functools.reduce(jnp.maximum, tiles, m_old)
        scale = jnp.exp(m_old - m_new)
        s, a, p = stat[1] * scale, stat[2] * scale, stat[3]
        for j, t in enumerate(tiles):
            e = jnp.exp(t - m_new)
            s += e
            a += e * t
            p += jnp.where(ids_rel == i * BLOCK + j * LANES, t, 0.0)
        stat[0], stat[1], stat[2], stat[3] = m_new, s, a, p

    fetch(0).wait()
    z_ref[...] = logits(0)

    def step(i, _):
        fetch(i).wait()
        nxt = i + DEPTH - 1

        @pl.when(nxt < steps)
        def _():
            fetch(nxt).start(priority=1)

        z = logits(i)
        fold(i - 1)
        z_ref[...] = z
        return 0

    lax.fori_loop(1, steps, step, 0)
    fold(steps - 1)

    m_t, s_t, a_t, p_t = stat[0].T, stat[1].T, stat[2].T, stat[3].T
    m = jnp.max(m_t, axis=0, keepdims=True)
    wgt = jnp.exp(m_t - m)
    for k, v in enumerate((m, jnp.sum(s_t * wgt, axis=0, keepdims=True),
                           jnp.sum(a_t * wgt, axis=0, keepdims=True), jnp.sum(p_t, axis=0, keepdims=True))):
        out_ref[k:k + 1, :pos] = v


def exchange_kernel(n_dev, mine, out_ref, got, send_sem, recv_sem):
    me = lax.axis_index("tp")
    barrier = pltpu.get_barrier_semaphore()
    for d in range(1, n_dev):
        pl.semaphore_signal(barrier, inc=1, device_id={"tp": lax.rem(me + d, n_dev)}, device_id_type=MESH)
    got[me] = mine[...]
    pl.semaphore_wait(barrier, n_dev - 1)

    def send(d):
        return pltpu.make_async_remote_copy(
            src_ref=mine, dst_ref=got.at[me], send_sem=send_sem.at[d], recv_sem=recv_sem.at[me],
            device_id={"tp": lax.rem(me + d, n_dev)}, device_id_type=MESH)

    def arrive(d):
        peer = lax.rem(me + d, n_dev)
        return pltpu.make_async_remote_copy(
            src_ref=mine, dst_ref=got.at[peer], send_sem=send_sem.at[d], recv_sem=recv_sem.at[peer],
            device_id={"tp": peer}, device_id_type=MESH)

    sends = [send(d) for d in range(1, n_dev)]
    for c in sends:
        c.start()
    for d in range(1, n_dev):
        arrive(d).wait_recv()
    all_m = [got[d, 0:1, :] for d in range(n_dev)]
    top = functools.reduce(jnp.maximum, all_m)
    wgt = [jnp.exp(v - top) for v in all_m]
    out_ref[0:1, :] = top
    out_ref[1:2, :] = sum(got[d, 1:2, :] * wgt[d] for d in range(n_dev))
    out_ref[2:3, :] = sum(got[d, 2:3, :] * wgt[d] for d in range(n_dev))
    out_ref[3:4, :] = sum(got[d, 3:4, :] for d in range(n_dev))
    for c in sends:
        c.wait_send()


def solution(mesh):
    n_dev = mesh.shape["tp"]

    def local_part(hidden, norm_w, embedding, draft_ids):
        _, pos, width = hidden.shape
        hbm = pl.BlockSpec(memory_space=pltpu.HBM)
        vmem = pl.BlockSpec(memory_space=pltpu.VMEM)
        tile = pltpu.VMEM((8, LANES), jnp.float32)
        mine = pl.pallas_call(
            stream_kernel,
            out_shape=tile,
            in_specs=[hbm] * 4,
            out_specs=vmem,
            scratch_shapes=[
                pltpu.VMEM((1, pos, width), jnp.bfloat16),
                pltpu.VMEM((width // LANES, LANES), jnp.bfloat16),
                pltpu.VMEM((1, pos), jnp.int32),
                pltpu.VMEM((pos, width), jnp.bfloat16),
                pltpu.VMEM((DEPTH, BLOCK, width), jnp.bfloat16),
                pltpu.VMEM((pos, BLOCK), jnp.float32),
                pltpu.VMEM((4, pos, LANES), jnp.float32),
                pltpu.SemaphoreType.DMA((3,)),
                pltpu.SemaphoreType.DMA((DEPTH,)),
            ],
            compiler_params=pltpu.CompilerParams(vmem_limit_bytes=60 * 2**20),
            cost_estimate=pl.CostEstimate(flops=2 * pos * embedding.size, bytes_accessed=2 * embedding.size,
                                          transcendentals=pos * embedding.shape[0]),
            name="stream",
        )(hidden, norm_w.reshape(width // LANES, LANES), draft_ids, embedding)
        out = pl.pallas_call(
            functools.partial(exchange_kernel, n_dev),
            out_shape=tile,
            in_specs=[vmem],
            out_specs=vmem,
            scratch_shapes=[
                pltpu.VMEM((n_dev, 8, LANES), jnp.float32),
                pltpu.SemaphoreType.DMA((n_dev,)),
                pltpu.SemaphoreType.DMA((n_dev,)),
            ],
            compiler_params=pltpu.CompilerParams(collective_id=0, has_side_effects=True),
            name="exchange",
        )(mine)
        top, total, weighted, picked = (out[k:k + 1, :pos] for k in range(4))
        log_norm = top + jnp.log(total)
        return picked - log_norm, log_norm - weighted / total

    return jax.shard_map(local_part, mesh=mesh,
                         in_specs=(P("dp", None, None), P(None), P("tp", None), P("dp", None)),
                         out_specs=(P("dp", None), P("dp", None)), check_vma=False)
```

time: 54.3 us -> 49.8 us (0.917)
  Pallas kernels: 53 us -> 47.9 us
  local copies, waits for them, and re-layouts: 0 us -> 0.58 us
    pallas_call x1 -> x2, Pallas kernels: 53 us -> 47.9 us  [the longest x1 40.5 us: local_part(): pl.pallas_call(stream_kernel, out_shape=tile, in_specs=[hbm] * 4, out_spe...]
    unnamed x0 -> x2, local copies, waits for them, and re-layouts: none -> 0.58 us
where the time goes in v3:
time: 49.8 us; the launch traced here: 49.7 us
  Pallas kernels  47.9 us (96%)
  between operations  0.65 us (1%)
  local copies, waits for them, and re-layouts  0.58 us (1%)
  other arithmetic  0.53 us (1%)
    pallas_call x1, Pallas kernels, local_part(): pl.pallas_call(stream_kernel, out_shape=tile, in_specs=[hbm] * 4, out_spe...  40.5 us
    pallas_call x1, Pallas kernels, local_part(): pl.pallas_call(functools.partial(exchange_kernel, n_dev), out_shape=tile,...  7.39 us

profile of v3, /device:TPU:0, one launch (start us, length us, event | category | flops | bytes accessed | tf_op | source)
XLA Modules:
  0.0 49.7 jit_solution(15261392892878519148)
XLA Ops:
  0.6 40.5 %stream.1.mine = f32[8,128]{1,0:T(8,128)S(1)} custom-call(bf16[1,16,2048]{2,1,0:T(8,128)(2,1)} %x_hbm.1, bf16[16,128]{1,0:T(8,128)(2,1)} %bitcast.1, s32[1,16]{1,0:T(1,128)} %ids_hbm.1, bf16[32000,2048]{1,0:T(8,128)(2,1)} %e_hbm.1), custom_call_target="tpu_custom_call" | custom-call | flops 2097152000 | bytes 131072000 | tf_op jit(solution)/shard_map/stream/pallas_call | solution.py:141
  41.2 0.0 copy-start
  41.2 0.6 %copy-done = f32[8,128]{1,0:T(8,128)} copy-done((f32[8,128]{1,0:T(8,128)}, f32[8,128]{1,0:T(8,128)S(1)}, u32[]{:S(2)}) %copy-start) | copy-done | bytes 4120
  41.8 7.4 %exchange.1 = f32[8,128]{1,0:T(8,128)S(1)} custom-call(f32[8,128]{1,0:T(8,128)} %copy-done), custom_call_target="tpu_custom_call" | custom-call | tf_op jit(solution)/shard_map/exchange/pallas_call | solution.py:162
  49.2 0.5 %divide_subtract_fusion = (f32[1,16]{1,0:T(1,128)}, f32[1,16]{1,0:T(1,128)}) fusion(f32[8,128]{1,0:T(8,128)S(1)} %exchange.1), kind=kLoop, calls=%fused_computation | loop fusion | flops 64 | bytes 384 | tf_op jit(solution)/shard_map/sub | solution.py:177
Async XLA Ops:
  41.2 0.6 %copy-start = (f32[8,128]{1,0:T(8,128)}, f32[8,128]{1,0:T(8,128)S(1)}, u32[]{:S(2)}) copy-start(f32[8,128]{1,0:T(8,128)S(1)} %stream.1.mine) | copy-start | bytes 12292

commit v4 on v3

--- a/solution.py
+++ b/solution.py
@@ -171,7 +171,7 @@
             ],
             compiler_params=pltpu.CompilerParams(collective_id=0, has_side_effects=True),
             name="exchange",
-        )(mine)
+        )(pltpu.with_memory_space_constraint(mine, pltpu.VMEM))
         top, total, weighted, picked = (out[k:k + 1, :pos] for k in range(4))
         log_norm = top + jnp.log(total)
         return picked - log_norm, log_norm - weighted / total

time: 49.8 us -> 48.5 us (0.974)
  Pallas kernels: 47.9 us -> 47.3 us
  local copies, waits for them, and re-layouts: 0.58 us -> 0 us
    pallas_call x1, Pallas kernels: 7.39 us -> 6.75 us  [local_part(): pl.pallas_call(functools.partial(exchange_kernel, n_dev), out_shape=tile,...]
    unnamed x2 -> x0, local copies, waits for them, and re-layouts: 0.58 us -> none
where the time goes in v4:
time: 48.5 us
  Pallas kernels  47.3 us (98%)
  between operations  0.65 us (1%)
  other arithmetic  0.53 us (1%)
    pallas_call x1, Pallas kernels, local_part(): pl.pallas_call(stream_kernel, out_shape=tile, in_specs=[hbm] * 4, out_spe...  40.5 us
    pallas_call x1, Pallas kernels, local_part(): pl.pallas_call(functools.partial(exchange_kernel, n_dev), out_shape=tile,...  6.75 us

profile of v4, /device:TPU:0, one launch (start us, length us, event | category | flops | bytes accessed | tf_op | source)
XLA Modules:
  0.0 48.5 jit_solution(16851278499569496786)
XLA Ops:
  0.6 40.5 %stream.1.mine = f32[8,128]{1,0:T(8,128)S(1)} custom-call(bf16[1,16,2048]{2,1,0:T(8,128)(2,1)} %x_hbm.1, bf16[16,128]{1,0:T(8,128)(2,1)} %bitcast.1, s32[1,16]{1,0:T(1,128)} %ids_hbm.1, bf16[32000,2048]{1,0:T(8,128)(2,1)} %e_hbm.1), custom_call_target="tpu_custom_call" | custom-call | flops 2097152000 | bytes 131072000 | tf_op jit(solution)/shard_map/stream/pallas_call | solution.py:141
  41.2 6.7 %exchange.1 = f32[8,128]{1,0:T(8,128)S(1)} custom-call(f32[8,128]{1,0:T(8,128)S(1)} %stream.1.mine), custom_call_target="tpu_custom_call" | custom-call | tf_op jit(solution)/shard_map/exchange/pallas_call | solution.py:162
  47.9 0.5 %divide_subtract_fusion = (f32[1,16]{1,0:T(1,128)}, f32[1,16]{1,0:T(1,128)}) fusion(f32[8,128]{1,0:T(8,128)S(1)} %exchange.1), kind=kLoop, calls=%fused_computation | loop fusion | flops 64 | bytes 384 | tf_op jit(solution)/shard_map/sub | solution.py:177

commit v5 on v2

--- a/solution.py
+++ b/solution.py
@@ -8,61 +8,75 @@
 
 EPS = 1e-6
 LANES = 128
-BLOCK = 1280
-DEPTH = 8
+BLOCK = 512
+TILE = 256
+FLIP = 1024
+DEPTH = 20
+EARLY = 3
 LOW = -3.0e38
 MESH = pl.DeviceIdType.MESH
 
 
 def head_kernel(n_dev, x_hbm, w_hbm, ids_hbm, e_hbm, out_ref,
-                x_ref, w_ref, ids_ref, h_ref, buf, z_ref, stat, mine, got,
-                small_sem, ring_sem, send_sem, recv_sem):
-    rows = e_hbm.shape[0]
+                x_ref, w_ref, ids_ref, h_ref, odd, buf, flip, z_ref, stat, mine, got,
+                small_sem, odd_sem, ring_sem, send_sem, recv_sem):
+    rows, width = e_hbm.shape
     pos = x_ref.shape[1]
-    steps = rows // BLOCK
+    lead = odd.shape[0]
+    steps = (rows - lead) // BLOCK
     me = lax.axis_index("tp")
     barrier = pltpu.get_barrier_semaphore()
 
     small = [pltpu.make_async_copy(s, d, small_sem.at[k])
              for k, (s, d) in enumerate(((x_hbm, x_ref), (w_hbm, w_ref), (ids_hbm, ids_ref)))]
-    for c in small:
-        c.start()
+    first = pltpu.make_async_copy(e_hbm.at[pl.ds(0, lead), :], odd, odd_sem)
 
     def fetch(i):
         slot = lax.rem(i, DEPTH)
-        return pltpu.make_async_copy(e_hbm.at[pl.ds(i * BLOCK, BLOCK), :], buf.at[slot], ring_sem.at[slot])
+        return pltpu.make_async_copy(e_hbm.at[pl.ds(lead + i * BLOCK, BLOCK), :], buf.at[slot], ring_sem.at[slot])
 
-    for i in range(DEPTH - 1):
+    first.start()
+    for i in range(EARLY):
         fetch(i).start()
+    for c in small:
+        c.start()
     for d in range(1, n_dev):
         pl.semaphore_signal(barrier, inc=1, device_id={"tp": lax.rem(me + d, n_dev)}, device_id_type=MESH)
     for c in small:
         c.wait()
+    for i in range(EARLY, DEPTH):
+        fetch(i).start()
 
     x = x_ref[0].astype(jnp.float32)
     r = lax.rsqrt(jnp.mean(x * x, axis=-1, keepdims=True) + EPS)
     gain = 1.0 + w_ref[...].astype(jnp.float32)
-    for c in range(x.shape[1] // LANES):
+    for c in range(width // LANES):
         cols = slice(c * LANES, (c + 1) * LANES)
         h_ref[:, cols] = (x[:, cols] * r * gain[c:c + 1, :]).astype(jnp.bfloat16)
 
     sub = lax.broadcasted_iota(jnp.int32, (pos, pos), 0)
     lan = lax.broadcasted_iota(jnp.int32, (pos, pos), 1)
-    eye = sub == lan
     ids_row = jnp.broadcast_to(ids_ref[...], (pos, pos)).astype(jnp.float32)
-    ids_col = jnp.sum(jnp.where(eye, ids_row, 0.0), axis=1, keepdims=True).astype(jnp.int32)
+    ids_col = jnp.sum(jnp.where(sub == lan, ids_row, 0.0), axis=1, keepdims=True).astype(jnp.int32)
     ids_rel = ids_col - me * rows - lax.broadcasted_iota(jnp.int32, (pos, LANES), 1)
 
     stat[0] = jnp.full((pos, LANES), LOW, jnp.float32)
     for k in range(1, 4):
         stat[k] = jnp.zeros((pos, LANES), jnp.float32)
 
-    def logits(i):
-        return lax.dot_general(h_ref[...], buf[lax.rem(i, DEPTH)], (((1,), (1,)), ((), ())),
-                               preferred_element_type=jnp.float32)
+    def logits(src, count):
+        out = []
+        for j in range(count // TILE):
+            part = pl.ds(j * TILE, TILE)
+            turned = flip.at[j % 2]
+            turned[...] = src[part, 0:FLIP].T
+            z = jnp.dot(h_ref[:, 0:FLIP], turned[...], preferred_element_type=jnp.float32)
+            z += lax.dot_general(h_ref[:, FLIP:], src[part, FLIP:], (((1,), (1,)), ((), ())),
+                                 preferred_element_type=jnp.float32)
+            out += [z[:, c * LANES:(c + 1) * LANES] for c in range(TILE // LANES)]
+        return out
 
-    def fold(i):
-        tiles = [z_ref[:, j * LANES:(j + 1) * LANES] for j in range(BLOCK // LANES)]
+    def fold(tiles, start):
         m_old = stat[0]
         m_new = functools.reduce(jnp.maximum, tiles, m_old)
         scale = jnp.exp(m_old - m_new)
@@ -71,12 +85,14 @@
             e = jnp.exp(t - m_new)
             s += e
             a += e * t
-            p += jnp.where(ids_rel == i * BLOCK + j * LANES, t, 0.0)
+            p += jnp.where(ids_rel == start + j * LANES, t, 0.0)
         stat[0], stat[1], stat[2], stat[3] = m_new, s, a, p
 
-    fetch(DEPTH - 1).start()
+    first.wait()
+    fold(logits(odd, lead), 0)
     fetch(0).wait()
-    z_ref[...] = logits(0)
+    for j, t in enumerate(logits(buf.at[0], BLOCK)):
+        z_ref[j] = t
 
     def step(i, _):
         fetch(i).wait()
@@ -86,16 +102,16 @@
         def _():
             fetch(nxt).start()
 
-        z = logits(i)
-        fold(i - 1)
-        z_ref[...] = z
+        tiles = logits(buf.at[lax.rem(i, DEPTH)], BLOCK)
+        fold([z_ref[j] for j in range(BLOCK // LANES)], lead + (i - 1) * BLOCK)
+        for j, t in enumerate(tiles):
+            z_ref[j] = t
         return 0
 
     lax.fori_loop(1, steps, step, 0)
-    fold(steps - 1)
+    fold([z_ref[j] for j in range(BLOCK // LANES)], lead + (steps - 1) * BLOCK)
 
-    m_l, s_l, a_l, p_l = stat[0], stat[1], stat[2], stat[3]
-    m_t, s_t, a_t, p_t = m_l.T, s_l.T, a_l.T, p_l.T
+    m_t, s_t, a_t, p_t = stat[0].T, stat[1].T, stat[2].T, stat[3].T
     m = jnp.max(m_t, axis=0, keepdims=True)
     wgt = jnp.exp(m_t - m)
     for k, v in enumerate((m, jnp.sum(s_t * wgt, axis=0, keepdims=True),
@@ -105,10 +121,9 @@
     pl.semaphore_wait(barrier, n_dev - 1)
 
     def send(d):
-        peer = lax.rem(me + d, n_dev)
         return pltpu.make_async_remote_copy(
             src_ref=mine, dst_ref=got.at[me], send_sem=send_sem.at[d], recv_sem=recv_sem.at[me],
-            device_id={"tp": peer}, device_id_type=MESH)
+            device_id={"tp": lax.rem(me + d, n_dev)}, device_id_type=MESH)
 
     def arrive(d):
         peer = lax.rem(me + d, n_dev)
@@ -121,14 +136,13 @@
         c.start()
     for d in range(1, n_dev):
         arrive(d).wait_recv()
-    ms = [got[d, 0:1, :pos] for d in range(n_dev)]
-    top = functools.reduce(jnp.maximum, ms)
-    ws = [jnp.exp(v - top) for v in ms]
-    total = sum(got[d, 1:2, :pos] * ws[d] for d in range(n_dev))
-    weighted = sum(got[d, 2:3, :pos] * ws[d] for d in range(n_dev))
-    picked = sum(got[d, 3:4, :pos] for d in range(n_dev))
-    for k, v in enumerate((top, total, weighted, picked)):
-        out_ref[k:k + 1, :pos] = v
+    all_m = [got[d, 0:1, :pos] for d in range(n_dev)]
+    top = functools.reduce(jnp.maximum, all_m)
+    wgt = [jnp.exp(v - top) for v in all_m]
+    out_ref[0:1, :pos] = top
+    out_ref[1:2, :pos] = sum(got[d, 1:2, :pos] * wgt[d] for d in range(n_dev))
+    out_ref[2:3, :pos] = sum(got[d, 2:3, :pos] * wgt[d] for d in range(n_dev))
+    out_ref[3:4, :pos] = sum(got[d, 3:4, :pos] for d in range(n_dev))
     for c in sends:
         c.wait_send()
 
@@ -150,12 +164,15 @@
                 pltpu.VMEM((width // LANES, LANES), jnp.bfloat16),
                 pltpu.VMEM((1, pos), jnp.int32),
                 pltpu.VMEM((pos, width), jnp.bfloat16),
+                pltpu.VMEM((embedding.shape[0] % BLOCK, width), jnp.bfloat16),
                 pltpu.VMEM((DEPTH, BLOCK, width), jnp.bfloat16),
-                pltpu.VMEM((pos, BLOCK), jnp.float32),
+                pltpu.VMEM((2, FLIP, TILE), jnp.bfloat16),
+                pltpu.VMEM((BLOCK // LANES, pos, LANES), jnp.float32),
                 pltpu.VMEM((4, pos, LANES), jnp.float32),
                 pltpu.VMEM((8, LANES), jnp.float32),
                 pltpu.VMEM((n_dev, 8, LANES), jnp.float32),
                 pltpu.SemaphoreType.DMA((3,)),
+                pltpu.SemaphoreType.DMA,
                 pltpu.SemaphoreType.DMA((DEPTH,)),
                 pltpu.SemaphoreType.DMA((n_dev,)),
                 pltpu.SemaphoreType.DMA((n_dev,)),

time: 54.3 us -> 47.7 us (0.88)
  Pallas kernels: 53 us -> 46.5 us
    pallas_call x1, Pallas kernels: 53 us -> 46.5 us  [local_part(): pl.pallas_call(functools.partial(head_kernel, n_dev), out_shape=pltpu.VME...]
where the time goes in v5:
time: 47.7 us; the launch traced here: 47.6 us
  Pallas kernels  46.5 us (97%)
  between operations  0.64 us (1%)
  other arithmetic  0.53 us (1%)
    pallas_call x1, Pallas kernels, local_part(): pl.pallas_call(functools.partial(head_kernel, n_dev), out_shape=pltpu.VME...  46.5 us

profile of v5, /device:TPU:0, one launch (start us, length us, event | category | flops | bytes accessed | tf_op | source)
XLA Modules:
  0.0 47.6 jit_solution(8074502179946488023)
XLA Ops:
  0.6 46.5 %head.1 = f32[8,128]{1,0:T(8,128)S(1)} custom-call(bf16[1,16,2048]{2,1,0:T(8,128)(2,1)} %x_hbm.1, bf16[16,128]{1,0:T(8,128)(2,1)} %bitcast.1, s32[1,16]{1,0:T(1,128)} %ids_hbm.1, bf16[32000,2048]{1,0:T(8,128)(2,1)} %e_hbm.1), custom_call_target="tpu_custom_call" | custom-call | flops 2097152000 | bytes 131072000 | tf_op jit(solution)/shard_map/head/pallas_call | solution.py:157
  47.1 0.5 %divide_subtract_fusion = (f32[1,16]{1,0:T(1,128)}, f32[1,16]{1,0:T(1,128)}) fusion(f32[8,128]{1,0:T(8,128)S(1)} %head.1), kind=kLoop, calls=%fused_computation | loop fusion | flops 64 | bytes 384 | tf_op jit(solution)/shard_map/sub | solution.py:188

commit v6 on v5

--- a/solution.py
+++ b/solution.py
@@ -12,7 +12,6 @@
 TILE = 256
 FLIP = 1024
 DEPTH = 20
-EARLY = 3
 LOW = -3.0e38
 MESH = pl.DeviceIdType.MESH
 
@@ -35,17 +34,22 @@
         slot = lax.rem(i, DEPTH)
         return pltpu.make_async_copy(e_hbm.at[pl.ds(lead + i * BLOCK, BLOCK), :], buf.at[slot], ring_sem.at[slot])
 
-    first.start()
-    for i in range(EARLY):
-        fetch(i).start()
     for c in small:
         c.start()
+
+    def prime(i, _):
+        @pl.when(i == 0)
+        def _():
+            first.start()
+
+        fetch(i).start()
+        return 0
+
+    lax.fori_loop(0, DEPTH, prime, 0)
     for d in range(1, n_dev):
         pl.semaphore_signal(barrier, inc=1, device_id={"tp": lax.rem(me + d, n_dev)}, device_id_type=MESH)
     for c in small:
         c.wait()
-    for i in range(EARLY, DEPTH):
-        fetch(i).start()
 
     x = x_ref[0].astype(jnp.float32)
     r = lax.rsqrt(jnp.mean(x * x, axis=-1, keepdims=True) + EPS)

time: 47.7 us -> 47 us (0.985)
  Pallas kernels: 46.5 us -> 45.8 us
    pallas_call x1, Pallas kernels: 46.5 us -> 45.8 us  [local_part(): pl.pallas_call(functools.partial(head_kernel, n_dev), out_shape=pltpu.VME...]
where the time goes in v6:
time: 47 us; the launch traced here: 46.9 us
  Pallas kernels  45.8 us (97%)
  between operations  0.64 us (1%)
  other arithmetic  0.53 us (1%)
    pallas_call x1, Pallas kernels, local_part(): pl.pallas_call(functools.partial(head_kernel, n_dev), out_shape=pltpu.VME...  45.8 us

profile of v6, /device:TPU:0, one launch (start us, length us, event | category | flops | bytes accessed | tf_op | source)
XLA Modules:
  0.0 46.9 jit_solution(1430721217558048969)
XLA Ops:
  0.6 45.8 %head.1 = f32[8,128]{1,0:T(8,128)S(1)} custom-call(bf16[1,16,2048]{2,1,0:T(8,128)(2,1)} %x_hbm.1, bf16[16,128]{1,0:T(8,128)(2,1)} %bitcast.1, s32[1,16]{1,0:T(1,128)} %ids_hbm.1, bf16[32000,2048]{1,0:T(8,128)(2,1)} %e_hbm.1), custom_call_target="tpu_custom_call" | custom-call | flops 2097152000 | bytes 131072000 | tf_op jit(solution)/shard_map/head/pallas_call | solution.py:161
  46.4 0.5 %divide_subtract_fusion = (f32[1,16]{1,0:T(1,128)}, f32[1,16]{1,0:T(1,128)}) fusion(f32[8,128]{1,0:T(8,128)S(1)} %head.1), kind=kLoop, calls=%fused_computation | loop fusion | flops 64 | bytes 384 | tf_op jit(solution)/shard_map/sub | solution.py:192
